TPU v7x, 32 devices: a whole 2x2x4 slice. The times are simulated.
32 devices in a mesh: freq: 16 (over z, x, core), grid: 2 (over y).
Axes of the slice: x: 2, y: 2, z: 4, core: 2. Of those that a mesh axis runs over, the one named last changes fastest.
Arguments:
- cross_spectra: float32 [2, 32, 256, 256], P(None, None, 'freq', 'grid'), as said below
- sensor_modes: float32 [32, 96, 256], P('freq', None, 'grid'), may hold values from -0.375 to 0.375
- source_modes: float32 [32, 96, 256], P('freq', None, 'grid'), may hold values from -6 to 6
- wavenumber: float32 [32, 96], P('freq'), may hold values from 0.5 to 2
- attenuation: float32 [32, 96], P('freq'), may hold values from 0.002 to 0.03
- mode_counts: int32 [32], P('freq'), may hold values from 48 to 96
Outputs:
- bartlett_power: float32 [64, 256], P('freq', 'grid')
Inputs may be any that keep to these rules, and one draw needn't show every extreme that they name: `cross_spectra`: each bin's matrix K_f is Hermitian and positive definite. Modes with index mode_counts[f] or more are left out in bin f.
All inputs are finite; a program needn't handle non-finite values.
Results may differ from a plain program's by a relative error of at most 0.0003.
Values sent between devices are 32-bit elements; how exact they have to be, the bound alone decides.
A program may use at most 128 MiB of HBM per device.

v0:
```python
import jax
import jax.numpy as jnp
from jax import lax
from jax.sharding import PartitionSpec as P

RANGES = 64


HIGH = lax.Precision.HIGHEST


def replica_terms(wave_row, atten_row, count, source_row, ranges):
    phase = wave_row[:, None] * ranges[None, :]
    magnitude = jnp.exp(-atten_row[:, None] * ranges[None, :]) / jnp.sqrt(phase)
    keep = (jnp.arange(source_row.shape[0], dtype=jnp.int32) < count).astype(jnp.float32)
    hankel_real = magnitude * jnp.cos(phase) * keep[:, None]
    hankel_imag = magnitude * jnp.sin(phase) * keep[:, None]
    coef_real = hankel_real[:, :, None] * source_row[:, None, :]
    coef_imag = hankel_imag[:, :, None] * source_row[:, None, :]
    return (coef_real, coef_imag)


def per_device(cross_spectra, sensor_modes, source_modes, wavenumber, attenuation, mode_counts):
    modes = sensor_modes.shape[1]
    bins_here = sensor_modes.shape[0]
    depth_here = source_modes.shape[2]
    total_bins = bins_here * lax.axis_size("freq")
    whole_spectra = lax.all_to_all(
        lax.all_to_all(cross_spectra, "freq", split_axis=1, concat_axis=2, tiled=True),
        "grid",
        split_axis=1,
        concat_axis=3,
        tiled=True,
    )
    whole_modes = lax.all_to_all(sensor_modes, "grid", split_axis=0, concat_axis=2, tiled=True)
    product = jnp.einsum("cbij,bmj->cbim", whole_spectra, whole_modes, precision=HIGH)
    projected = jnp.einsum("bmi,cbin->cbmn", whole_modes, product, precision=HIGH)
    gram = jnp.einsum("bmi,bni->bmn", whole_modes, whole_modes, precision=HIGH)
    stacked_local = jnp.concatenate([projected, gram[None]], 0)
    spectra = lax.all_gather(stacked_local, "grid", axis=1, tiled=True)
    count = RANGES // lax.axis_size("freq") * lax.axis_size("freq")
    ranges = 1.0 + jnp.arange(count, dtype=jnp.int32).astype(jnp.float32)

    def one_bin(bin_index, total):
        block = spectra[:, bin_index]
        coupling = jnp.concatenate(
            [jnp.concatenate([block[0], -block[1]], 1), jnp.concatenate([block[1], block[0]], 1)], 0
        )
        coef_real, coef_imag = replica_terms(
            wavenumber[bin_index],
            attenuation[bin_index],
            mode_counts[bin_index],
            source_modes[bin_index],
            ranges,
        )
        coefs = jnp.concatenate([coef_real, coef_imag], 0).reshape(2 * modes, count * depth_here)
        image = jnp.dot(coupling, coefs, precision=HIGH)
        weighted = jnp.einsum(
            "mn,cnx->cmx", block[2], coefs.reshape(2, modes, count * depth_here), precision=HIGH
        )
        weighted = weighted.reshape(2 * modes, count * depth_here)
        numer = jnp.sum(coefs * image, axis=0)
        denom = jnp.sum(coefs * weighted, axis=0)
        return total + (numer / denom).reshape(count, depth_here)

    summed = lax.fori_loop(0, bins_here, one_bin, jnp.zeros((count, depth_here), jnp.float32))
    return lax.psum_scatter(summed / total_bins, "freq", scatter_dimension=0, tiled=True)


def solution(mesh):
    placed = (
        P(None, None, "freq", "grid"),
        P("freq", None, "grid"),
        P("freq", None, "grid"),
        P("freq", None),
        P("freq", None),
        P("freq"),
    )
    return jax.shard_map(
        per_device, mesh=mesh, in_specs=placed, out_specs=P("freq", "grid"), check_vma=False
    )
```

profile of v0, /device:TPU:0, one launch (start us, length us, event | category | flops | bytes accessed | tf_op | source)
XLA Modules:
  0.0 178.7 jit_solution(12962401052543887064)
XLA Ops:
  1.2 21.5 %all_to_all.48 = f32[2,32,16,128]{3,2,0,1:T(8,128)S(1)} all-to-all(f32[2,32,16,128]{3,2,0,1:T(8,128)S(1)} %copy.23), channel_id=1, replica_groups=mesh['freq'=16,'grid'=2] {'freq'}, dimensions={1} | all-to-all | bytes 1048576 | tf_op jit(solution)/shard_map/all_to_all | solution.py:29
  22.6 3.3 %all-to-all-start = ((f32[2,96,128]{2,1,0:T(8,128)}), f32[2,96,128]{2,1,0:T(8,128)S(1)}, u32[]{:S(2)}, u32[]{:S(2)}) async-start(f32[2,96,128]{2,1,0:T(8,128)} %param.9), calls=%async_computation | async-start | bytes 196608 | tf_op jit(solution)/shard_map/all_to_all | solution.py:35
  26.8 3.4 %all-to-all-done = f32[2,96,128]{2,1,0:T(8,128)S(1)} async-done(((f32[2,96,128]{2,1,0:T(8,128)}), f32[2,96,128]{2,1,0:T(8,128)S(1)}, u32[]{:S(2)}, u32[]{:S(2)}) %all-to-all-start) | async-done | bytes 98336 | tf_op jit(solution)/shard_map/all_to_all | solution.py:35
  30.3 3.5 %all-to-all-start.2 = ((f32[2,2,256,128]{3,2,0,1:T(8,128)}), f32[2,2,256,128]{3,2,0,1:T(8,128)S(1)}, u32[]{:S(2)}, u32[]{:S(2)}) async-start(f32[2,2,256,128]{3,2,0,1:T(8,128)} %bitcast.6), calls=%async_computation.2 | async-start | bytes 1048576 | tf_op jit(solution)/shard_map/all_to_all | solution.py:28
  36.2 5.0 %all-to-all-done.2 = f32[2,2,256,128]{3,2,0,1:T(8,128)S(1)} async-done(((f32[2,2,256,128]{3,2,0,1:T(8,128)}), f32[2,2,256,128]{3,2,0,1:T(8,128)S(1)}, u32[]{:S(2)}, u32[]{:S(2)}) %all-to-all-start.2) | async-done | bytes 524320 | tf_op jit(solution)/shard_map/all_to_all | solution.py:28
  42.2 5.8 %all_gather.3 = f32[3,2,96,96]{3,2,0,1:T(8,128)S(1)} all-gather(f32[3,1,96,96]{3,2,0,1:T(8,128)S(1)} %copy.28), channel_id=1, replica_groups=mesh['freq'=16,'grid'=2] {'grid'}, dimensions={1}, use_global_device_ids=true | all-gather | bytes 331776 | tf_op jit(solution)/shard_map/all_gather | solution.py:40
  48.1 72.4 %while.15 = (s32[]{:T(128)}, f32[64,128]{1,0:T(8,128)S(1)}, f32[2,96]{1,0:T(2,128)S(1)}, f32[2,96]{1,0:T(2,128)S(1)}, s32[2]{0:T(128)S(1)}, /*index=5*/f32[2,96,...) while((s32[]{:T(128)}, f32[64,128]{1,0:T(8,128)S(1)}, ...), condition=%wide.region_3.0_spmd.clone.clone, body=%wide.region_0.0_spmd.clone.clone.sunk | while | flops 5445426688 | bytes 89226920 | solution.py:66
  49.7 1.8 %broadcast_multiply_fusion.4 = (f32[96,64,128]{2,1,0:T(8,128)S(1)}, f32[96,64,128]{2,1,0:T(8,128)S(1)}) fusion(f32[96,64]{1,0:T(8,128)S(1)} %copy.48, f32[96,128]{1,0:T(8,128)S(1)} %dynamic-slice_bitcast_fusion.4, f32[96,64]{1,0:T(8,128)S(1)} %copy.49), kind=kLoop, calls=%fused_computation.9.clone.1 | loop fusion | flops 1572864 | bytes 6389760 | tf_op jit(solution)/shard_map/while/body/eval_jaxpr/mul | solution.py:19
  51.5 2.2 %bitcast_dynamic-update-slice_fusion.4 = f32[192,8192]{1,0:T(8,128)S(1)} fusion(f32[12,8,64,128]{3,2,1,0:T(8,128)S(1)} %bitcast.112), kind=kLoop, calls=%fused_computation.6.clone.1 | loop fusion | bytes 6291456 | tf_op jit(solution)/shard_map/while
  53.7 2.2 %bitcast_dynamic-update-slice_fusion.5 = f32[192,8192]{1,0:T(8,128)S(1)} fusion(f32[192,8192]{1,0:T(8,128)S(1)} %bitcast_dynamic-update-slice_fusion.4, f32[12,8,64,128]{3,2,1,0:T(8,128)S(1)} %bitcast.111), kind=kLoop, calls=%fused_computation.5.clone.1 | loop fusion | bytes 6291456 | tf_op jit(solution)/shard_map/while/body/eval_jaxpr/concatenate | solution.py:56
  55.9 2.6 %copy-done = f32[192,8192]{1,0:T(8,128)} copy-done((f32[192,8192]{1,0:T(8,128)}, f32[192,8192]{1,0:T(8,128)S(1)}, u32[]{:S(2)}) %copy-start) | copy-done | bytes 6291480 | tf_op jit(solution)/shard_map/while
  58.5 6.4 %fusion.44 = f32[8192]{0:T(1024)S(1)} fusion(f32[192,8192]{1,0:T(8,128)S(1)} %bitcast_dynamic-update-slice_fusion.5, f32[96,96]{1,0:T(8,128)S(1)} %get-tuple-element.301, f32[96,96]{1,0:T(8,128)S(1)} %get-tuple-element.302, f32[96,96]{1,0:T(8,128)S(1)} %fusion.43), kind=kOutput, calls=%fused_computation.8.clone.1 | convolution fusion | flops 3627126784 | bytes 6434816 | tf_op jit(solution)/shard_map/while/body/eval_jaxpr/dot_general | solution.py:57
  64.9 3.2 %pad_maximum_fusion.3 = f32[192,64,128]{2,1,0:T(8,128)} fusion(f32[96,64,128]{2,1,0:T(8,128)S(1)} %get-tuple-element.300, f32[96,64,128]{2,1,0:T(8,128)S(1)} %get-tuple-element.299), kind=kLoop, calls=%fused_computation.4.clone.1 | loop fusion | flops 1572864 | bytes 12582912 | tf_op jit(solution)/shard_map/while/body/eval_jaxpr/concatenate | solution.py:56
  68.0 7.2 %reshape.257 = f32[2,96,8192]{2,1,0:T(8,128)} reshape(f32[192,64,128]{2,1,0:T(8,128)} %pad_maximum_fusion.3) | data formatting | bytes 12582912 | tf_op jit(solution)/shard_map/while/body/eval_jaxpr/reshape;while/body/eval_jaxpr/reshape | solution.py:59
  75.2 9.0 %fusion.45 = f32[8192]{0:T(1024)S(1)} fusion(f32[2,96,8192]{2,1,0:T(8,128)} %bitcast.110, f32[2,96,8192]{2,1,0:T(8,128)} %reshape.257, f32[3,1,96,96]{3,2,1,0:T(8,128)S(1)} %dynamic-slice_bitcast_fusion.5), kind=kOutput, calls=%fused_computation.7.clone.1 | convolution fusion | flops 1815076864 | bytes 12664832 | tf_op jit(solution)/shard_map/while/body/eval_jaxpr/mn,cnx->cmx/dot_general | solution.py:58
  85.8 1.8 %broadcast_multiply_fusion.4 = (f32[96,64,128]{2,1,0:T(8,128)S(1)}, f32[96,64,128]{2,1,0:T(8,128)S(1)}) fusion(f32[96,64]{1,0:T(8,128)S(1)} %copy.48, f32[96,128]{1,0:T(8,128)S(1)} %dynamic-slice_bitcast_fusion.4, f32[96,64]{1,0:T(8,128)S(1)} %copy.49), kind=kLoop, calls=%fused_computation.9.clone.1 | loop fusion | flops 1572864 | bytes 6389760 | tf_op jit(solution)/shard_map/while/body/eval_jaxpr/mul | solution.py:19
  87.7 2.2 %bitcast_dynamic-update-slice_fusion.4 = f32[192,8192]{1,0:T(8,128)S(1)} fusion(f32[12,8,64,128]{3,2,1,0:T(8,128)S(1)} %bitcast.112), kind=kLoop, calls=%fused_computation.6.clone.1 | loop fusion | bytes 6291456 | tf_op jit(solution)/shard_map/while
  89.9 2.2 %bitcast_dynamic-update-slice_fusion.5 = f32[192,8192]{1,0:T(8,128)S(1)} fusion(f32[192,8192]{1,0:T(8,128)S(1)} %bitcast_dynamic-update-slice_fusion.4, f32[12,8,64,128]{3,2,1,0:T(8,128)S(1)} %bitcast.111), kind=kLoop, calls=%fused_computation.5.clone.1 | loop fusion | bytes 6291456 | tf_op jit(solution)/shard_map/while/body/eval_jaxpr/concatenate | solution.py:56
  92.1 2.6 %copy-done = f32[192,8192]{1,0:T(8,128)} copy-done((f32[192,8192]{1,0:T(8,128)}, f32[192,8192]{1,0:T(8,128)S(1)}, u32[]{:S(2)}) %copy-start) | copy-done | bytes 6291480 | tf_op jit(solution)/shard_map/while
  94.7 6.4 %fusion.44 = f32[8192]{0:T(1024)S(1)} fusion(f32[192,8192]{1,0:T(8,128)S(1)} %bitcast_dynamic-update-slice_fusion.5, f32[96,96]{1,0:T(8,128)S(1)} %get-tuple-element.301, f32[96,96]{1,0:T(8,128)S(1)} %get-tuple-element.302, f32[96,96]{1,0:T(8,128)S(1)} %fusion.43), kind=kOutput, calls=%fused_computation.8.clone.1 | convolution fusion | flops 3627126784 | bytes 6434816 | tf_op jit(solution)/shard_map/while/body/eval_jaxpr/dot_general | solution.py:57
  101.1 3.2 %pad_maximum_fusion.3 = f32[192,64,128]{2,1,0:T(8,128)} fusion(f32[96,64,128]{2,1,0:T(8,128)S(1)} %get-tuple-element.300, f32[96,64,128]{2,1,0:T(8,128)S(1)} %get-tuple-element.299), kind=kLoop, calls=%fused_computation.4.clone.1 | loop fusion | flops 1572864 | bytes 12582912 | tf_op jit(solution)/shard_map/while/body/eval_jaxpr/concatenate | solution.py:56
  104.2 7.2 %reshape.257 = f32[2,96,8192]{2,1,0:T(8,128)} reshape(f32[192,64,128]{2,1,0:T(8,128)} %pad_maximum_fusion.3) | data formatting | bytes 12582912 | tf_op jit(solution)/shard_map/while/body/eval_jaxpr/reshape;while/body/eval_jaxpr/reshape | solution.py:59
  111.4 9.0 %fusion.45 = f32[8192]{0:T(1024)S(1)} fusion(f32[2,96,8192]{2,1,0:T(8,128)} %bitcast.110, f32[2,96,8192]{2,1,0:T(8,128)} %reshape.257, f32[3,1,96,96]{3,2,1,0:T(8,128)S(1)} %dynamic-slice_bitcast_fusion.5), kind=kOutput, calls=%fused_computation.7.clone.1 | convolution fusion | flops 1815076864 | bytes 12664832 | tf_op jit(solution)/shard_map/while/body/eval_jaxpr/mn,cnx->cmx/dot_general | solution.py:58
  120.4 57.6 %all-reduce = f32[64,128]{1,0:T(8,128)S(1)} all-reduce(f32[64,128]{1,0:T(8,128)S(1)} %broadcast_multiply_fusion.2), channel_id=2, replica_groups=mesh['freq'=16,'grid'=2] {'freq'}, use_global_device_ids=true, to_apply=%region_4.0.clone | all-reduce | flops 8192 | bytes 65536
  (47 shorter events, 8.5 us)
Async XLA Ops:
  0.0 48.0 %copy-start.2 = (f32[2,96]{1,0:T(2,128)S(1)}, f32[2,96]{1,0:T(2,128)}, u32[]{:S(2)}) copy-start(f32[2,96]{1,0:T(2,128)} %param.12) | copy-start | bytes 2308
  0.0 48.0 %copy-start.3 = (f32[2,96]{1,0:T(2,128)S(1)}, f32[2,96]{1,0:T(2,128)}, u32[]{:S(2)}) copy-start(f32[2,96]{1,0:T(2,128)} %param.11) | copy-start | bytes 2308
  0.0 48.0 %copy-start.4 = (s32[2]{0:T(128)S(1)}, s32[2]{0:T(128)}, u32[]{:S(2)}) copy-start(s32[2]{0:T(128)} %param.13) | copy-start | bytes 28
  0.0 48.0 %copy-start.1 = (f32[2,96,128]{2,1,0:T(8,128)S(1)}, f32[2,96,128]{2,1,0:T(8,128)}, u32[]{:S(2)}) copy-start(f32[2,96,128]{2,1,0:T(8,128)} %param.10) | copy-start | bytes 294916
  22.6 7.6 %all-to-all-start = ((f32[2,96,128]{2,1,0:T(8,128)}), f32[2,96,128]{2,1,0:T(8,128)S(1)}, u32[]{:S(2)}, u32[]{:S(2)}) async-start(f32[2,96,128]{2,1,0:T(8,128)} %param.9), calls=%async_computation | async-start | bytes 196608 | tf_op jit(solution)/shard_map/all_to_all | solution.py:35
  30.3 10.9 %all-to-all-start.2 = ((f32[2,2,256,128]{3,2,0,1:T(8,128)}), f32[2,2,256,128]{3,2,0,1:T(8,128)S(1)}, u32[]{:S(2)}, u32[]{:S(2)}) async-start(f32[2,2,256,128]{3,2,0,1:T(8,128)} %bitcast.6), calls=%async_computation.2 | async-start | bytes 1048576 | tf_op jit(solution)/shard_map/all_to_all | solution.py:28
  55.9 2.6 %copy-start = (f32[192,8192]{1,0:T(8,128)}, f32[192,8192]{1,0:T(8,128)S(1)}, u32[]{:S(2)}) copy-start(f32[192,8192]{1,0:T(8,128)S(1)} %bitcast_dynamic-update-slice_fusion.5) | copy-start | bytes 18874372 | tf_op jit(solution)/shard_map/while
  92.0 2.6 %copy-start = (f32[192,8192]{1,0:T(8,128)}, f32[192,8192]{1,0:T(8,128)S(1)}, u32[]{:S(2)}) copy-start(f32[192,8192]{1,0:T(8,128)S(1)} %bitcast_dynamic-update-slice_fusion.5) | copy-start | bytes 18874372 | tf_op jit(solution)/shard_map/while
where the time goes:
time: 179 us
  blocking collectives  84.9 us (47%)
  local copies, waits for them, and re-layouts  34 us (19%)
  matrix products  31.9 us (18%)
  other arithmetic  11.6 us (6%)
  waiting for transfers between devices  8.41 us (5%)
  starting transfers between devices  6.83 us (4%)
    unnamed x1, blocking collectives  57.6 us
    all_to_all x1, blocking collectives, per_device(): lax.all_to_all(cross_spectra, 'freq', split_axis=1, concat_axis=2, tiled=...  21.5 us
    dot_general x2, matrix products, one_bin(): jnp.einsum('mn,cnx->cmx', block[2], coefs.reshape(2, modes, count * depth...  18 us
    reshape x2, local copies, waits for them, and re-layouts, one_bin(): coefs.reshape(2, modes, count * depth_here)  14.3 us
    dot_general x2, matrix products, one_bin(): image = jnp.dot(coupling, coefs, precision=HIGH)  12.7 us
    while x6, local copies, waits for them, and re-layouts  9.54 us
    concatenate x2, other arithmetic, one_bin(): jnp.concatenate([coef_real, coef_imag], 0)  6.34 us
    all_gather x1, blocking collectives, per_device(): spectra = lax.all_gather(stacked_local, 'grid', axis=1, tiled=True)  5.81 us
  transfers between devices with their start and end apart: 2, of which 2 were waited for; matrix products, arithmetic and copies ran while one was open for 1% of the time, Pallas kernels for 0%

commit v1 on v0

v1 whole, which is shorter than its diff:
```python
import functools

import jax
import jax.numpy as jnp
from jax import lax
from jax.experimental import pallas as pl
from jax.experimental.pallas import tpu as pltpu
from jax.sharding import PartitionSpec as P

RANGES = 64
BLOCK = 8
LANES = 128

HIGH = lax.Precision.HIGHEST
MESH = pl.DeviceIdType.MESH
NT = (((1,), (1,)), ((), ()))


def kernel(
    nf, ng,
    spectra_hbm, sensor_hbm, source_hbm, wave_ref, atten_ref, counts_ref,
    out_ref,
    raw, outgoing, table, shapes, sources, shapes_wide, halves, weight, rows_scr, cols_scr, row_in,
    u_scr, v_scr, lhs, denom, power, parts,
    raw_sem, own_sem, mode_send, mode_recv, send_sem, recv_sem, part_send, part_recv,
):
    devices = nf * ng
    bins = outgoing.shape[0]
    nb = bins // devices
    row_count, col_count = raw.shape[2], raw.shape[3]
    modes = shapes.shape[2]
    ranges = u_scr.shape[1]
    share = ranges // nf
    depth_here = sources.shape[3]
    my_f, my_g = lax.axis_index("freq"), lax.axis_index("grid")
    me = my_f * ng + my_g

    raw_copy = pltpu.make_async_copy(spectra_hbm, raw, raw_sem)
    raw_copy.start()
    own = pl.ds(my_g * nb, nb)
    own_shapes = pltpu.make_async_copy(sensor_hbm.at[own], shapes.at[my_g], own_sem.at[0])
    own_sources = pltpu.make_async_copy(source_hbm.at[own], sources.at[my_g], own_sem.at[1])
    own_shapes.start()
    own_sources.start()

    barrier = pltpu.get_barrier_semaphore()

    def greet(k, carry):
        peer = lax.rem(me + k, devices)
        pl.semaphore_signal(
            barrier, inc=1, device_id=(peer // ng, lax.rem(peer, ng)), device_id_type=MESH
        )
        return carry

    lax.fori_loop(1, devices, greet, 0)

    raw_copy.wait()
    outgoing[...] = raw[0] + raw[1]
    my_rows = pl.ds(pl.multiple_of(my_f * row_count, row_count), row_count)
    for b in range(nb):
        table[my_g, b, my_rows, :] = outgoing[me * nb + b]

    pl.semaphore_wait(barrier, devices - 1)

    def mode_copies(k):
        peer = lax.rem(my_g + k, ng)
        theirs = pl.ds(peer * nb, nb)
        return [
            pltpu.make_async_remote_copy(
                src_ref=hbm.at[theirs],
                dst_ref=here.at[my_g],
                send_sem=mode_send.at[i, k],
                recv_sem=mode_recv.at[i, k],
                device_id=(my_f, peer),
                device_id_type=MESH,
            )
            for i, (hbm, here) in enumerate(((sensor_hbm, shapes), (source_hbm, sources)))
        ]

    for k in range(1, ng):
        for copy in mode_copies(k):
            copy.start()

    def piece(k):
        peer = lax.rem(me + k, devices)
        return pltpu.make_async_remote_copy(
            src_ref=outgoing.at[pl.ds(peer * nb, nb)],
            dst_ref=table.at[my_g, :, my_rows, :],
            send_sem=send_sem.at[k],
            recv_sem=recv_sem.at[k],
            device_id=(peer // ng, lax.rem(peer, ng)),
            device_id_type=MESH,
        )

    def send_piece(k, carry):
        piece(k).start()
        return carry

    lax.fori_loop(1, devices, send_piece, 0)

    for b in range(nb):
        row = my_g * nb + b
        row_in[...] = jnp.ones_like(row_in)
        row_in[0:1, 0:modes] = wave_ref[pl.ds(row, 1), :]
        row_in[1:2, 0:modes] = atten_ref[pl.ds(row, 1), :]
        radius = 1.0 + lax.broadcasted_iota(jnp.int32, (ranges, LANES), 0).astype(jnp.float32)
        lane = lax.broadcasted_iota(jnp.int32, (ranges, LANES), 1)
        phase = radius * row_in[0:1, :]
        magnitude = jnp.exp(-row_in[1:2, :] * radius) / jnp.sqrt(phase)
        magnitude = jnp.where(lane < counts_ref[row], magnitude, 0.0)
        filler = jnp.zeros((LANES - ranges, LANES), jnp.float32)
        for i, factor in enumerate((magnitude * jnp.cos(phase), magnitude * jnp.sin(phase))):
            rows_scr[b, i] = factor
            turned = jnp.concatenate([factor, filler], 0).T
            for blk in range(ranges // BLOCK):
                cols_scr[b, i, blk] = turned[0:modes, blk * BLOCK : (blk + 1) * BLOCK]

    own_shapes.wait()
    own_sources.wait()
    for k in range(1, ng):
        for copy in mode_copies(k):
            copy.wait_recv()

    shapes_wide[...] = jnp.zeros_like(shapes_wide)
    halves[...] = jnp.zeros_like(halves)
    for b in range(nb):
        for g in range(ng):
            shapes_wide[b, 0:modes, g * col_count : (g + 1) * col_count] = shapes[g, b]
            exact = sources[g, b]
            rounded = exact.astype(jnp.bfloat16)
            at = slice(g * depth_here, (g + 1) * depth_here)
            halves[b, 0:modes, at] = rounded
            halves[b, LANES : LANES + modes, at] = rounded
            weight[b, :, at] = 2.0 * exact - rounded.astype(jnp.float32)

    def put(k, block):
        high = block.astype(jnp.bfloat16)
        low = (block - high.astype(jnp.float32)).astype(jnp.bfloat16)
        lhs[k * modes : (k + 1) * modes, 0:LANES] = high
        lhs[k * modes : (k + 1) * modes, LANES : 2 * LANES] = low

    def forms(b):
        image = jnp.dot(lhs[...], halves[b], preferred_element_type=jnp.float32)
        image = image.reshape(BLOCK, modes, image.shape[1]) * weight[b][None]
        return jnp.sum(image, axis=1)

    for b in range(nb):
        wide = shapes_wide[b]
        gram = lax.dot_general(
            wide[0:modes], wide, NT, precision=HIGH, preferred_element_type=jnp.float32
        )

        def denom_block(blk, carry):
            first = pl.multiple_of(blk * BLOCK, BLOCK)
            row_real = rows_scr[b, 0, pl.ds(first, BLOCK), :]
            row_imag = rows_scr[b, 1, pl.ds(first, BLOCK), :]
            col_real, col_imag = cols_scr[b, 0, blk], cols_scr[b, 1, blk]
            for k in range(BLOCK):
                nr, ni = row_real[k : k + 1, :], row_imag[k : k + 1, :]
                mr = jnp.broadcast_to(col_real[:, k : k + 1], (modes, LANES))
                mi = jnp.broadcast_to(col_imag[:, k : k + 1], (modes, LANES))
                u = mr * nr + mi * ni
                u_scr[b, first + k] = u
                v_scr[b, first + k] = mr * ni - mi * nr
                put(k, gram * u)
            denom[b, pl.ds(first, BLOCK), :] = forms(b)
            return carry

        lax.fori_loop(0, ranges // BLOCK, denom_block, 0)

    def take_piece(k, carry):
        piece(k).wait_recv()
        return carry

    lax.fori_loop(1, devices, take_piece, 0)

    for b in range(nb):
        wide = shapes_wide[b]
        whole = jnp.concatenate([table[g, b] for g in range(ng)], axis=1)
        half = jnp.dot(wide, whole, precision=HIGH, preferred_element_type=jnp.float32)
        full = lax.dot_general(half, wide, NT, precision=HIGH, preferred_element_type=jnp.float32)
        turned = full.T
        even = (0.5 * (full + turned))[0:modes]
        odd = (0.5 * (full - turned))[0:modes]

        def numer_block(blk, carry):
            first = pl.multiple_of(blk * BLOCK, BLOCK)
            for k in range(BLOCK):
                put(k, even * u_scr[b, first + k] - odd * v_scr[b, first + k])
            score = forms(b) / (denom[b, pl.ds(first, BLOCK), :] * float(bins))
            for g in range(ng):
                for s in range(BLOCK // share):
                    value = score[s * share : (s + 1) * share, g * depth_here : (g + 1) * depth_here]
                    slot = blk * (BLOCK // share) + s
                    if b == 0:
                        power[g, slot] = value
                    else:
                        power[g, slot] += value
            return carry

        lax.fori_loop(0, ranges // BLOCK, numer_block, 0)

    def part(k):
        peer = lax.rem(me + k, devices)
        peer_f, peer_g = peer // ng, lax.rem(peer, ng)
        return pltpu.make_async_remote_copy(
            src_ref=power.at[peer_g, peer_f],
            dst_ref=parts.at[k],
            send_sem=part_send.at[k],
            recv_sem=part_recv.at[k],
            device_id=(peer_f, peer_g),
            device_id_type=MESH,
        )

    def send_part(k, carry):
        part(k).start()
        return carry

    lax.fori_loop(1, devices, send_part, 0)
    parts[0] = power[my_g, my_f]

    def finish(k, carry):
        piece(k).wait_send()
        part(k).wait()
        return carry

    for k in range(1, ng):
        for copy in mode_copies(k):
            copy.wait_send()
    lax.fori_loop(1, devices, finish, 0)
    out_ref[...] = jnp.sum(parts[...], axis=0)


def solution(mesh):
    nf, ng = mesh.shape["freq"], mesh.shape["grid"]
    devices = nf * ng

    def per_device(cross_spectra, sensor_modes, source_modes, wavenumber, attenuation, mode_counts):
        two, bins, rows, cols = cross_spectra.shape
        bins_here, modes, _ = sensor_modes.shape
        depth_here = source_modes.shape[2]
        nb = bins_here // ng
        ranges = RANGES // nf * nf
        share = ranges // nf
        f32, bf16 = jnp.float32, jnp.bfloat16
        dma = pltpu.SemaphoreType.DMA
        return pl.pallas_call(
            functools.partial(kernel, nf, ng),
            out_shape=jax.ShapeDtypeStruct((share, depth_here), f32),
            in_specs=[pl.BlockSpec(memory_space=pl.ANY)] * 3
            + [pl.BlockSpec(memory_space=pltpu.VMEM)] * 2
            + [pl.BlockSpec(memory_space=pltpu.SMEM)],
            out_specs=pl.BlockSpec(memory_space=pltpu.VMEM),
            scratch_shapes=[
                pltpu.VMEM((two, bins, rows, cols), f32),
                pltpu.VMEM((bins, rows, cols), f32),
                pltpu.VMEM((ng, nb, nf * rows, cols), f32),
                pltpu.VMEM((ng, nb, modes, cols), f32),
                pltpu.VMEM((ng, nb, modes, depth_here), f32),
                pltpu.VMEM((nb, LANES, ng * cols), f32),
                pltpu.VMEM((nb, 2 * LANES, ng * depth_here), bf16),
                pltpu.VMEM((nb, modes, ng * depth_here), f32),
                pltpu.VMEM((nb, 2, ranges, LANES), f32),
                pltpu.VMEM((nb, 2, ranges // BLOCK, modes, BLOCK), f32),
                pltpu.VMEM((8, LANES), f32),
                pltpu.VMEM((nb, ranges, modes, LANES), f32),
                pltpu.VMEM((nb, ranges, modes, LANES), f32),
                pltpu.VMEM((BLOCK * modes, 2 * LANES), bf16),
                pltpu.VMEM((nb, ranges, ng * depth_here), f32),
                pltpu.VMEM((ng, nf, share, depth_here), f32),
                pltpu.VMEM((devices, share, depth_here), f32),
                dma, dma((2,)), dma((2, ng)), dma((2, ng)),
                dma((devices,)), dma((devices,)), dma((devices,)), dma((devices,)),
            ],
            compiler_params=pltpu.CompilerParams(
                collective_id=0, has_side_effects=True, vmem_limit_bytes=60 * 1024 * 1024
            ),
        )(cross_spectra, sensor_modes, source_modes, wavenumber, attenuation, mode_counts)

    placed = (
        P(None, None, "freq", "grid"),
        P("freq", None, "grid"),
        P("freq", None, "grid"),
        P("freq", None),
        P("freq", None),
        P("freq"),
    )
    return jax.shard_map(
        per_device, mesh=mesh, in_specs=placed, out_specs=P("freq", "grid"), check_vma=False
    )
```

time: 179 us -> 29.1 us (0.16)
  blocking collectives: 84.9 us -> 0 us
  local copies, waits for them, and re-layouts: 34 us -> 1.26 us
  matrix products: 31.9 us -> 0 us
  Pallas kernels: 0 us -> 27.6 us
  other arithmetic: 11.6 us -> 0 us
  waiting for transfers between devices: 8.41 us -> 0 us
  starting transfers between devices: 6.83 us -> 0 us
    unnamed x1 -> x0, blocking collectives: 57.6 us -> none
    dot_general x7 -> x0, matrix products: 31.9 us -> none  [the longest x2 18 us: one_bin(): jnp.einsum('mn,cnx->cmx', block[2], coefs.reshape(2, modes, count * depth...]
    pallas_call x0 -> x1, Pallas kernels: none -> 27.6 us  [per_device(): pl.pallas_call(functools.partial(kernel, nf, ng), out_shape=jax.ShapeDtyp...]
    all_to_all x1 -> x0, blocking collectives: 21.5 us -> none  [per_device(): lax.all_to_all(cross_spectra, 'freq', split_axis=1, concat_axis=2, tiled=...]
    reshape x2 -> x0, local copies, waits for them, and re-layouts: 14.3 us -> none  [one_bin(): coefs.reshape(2, modes, count * depth_here)]
    while x6 -> x0, local copies, waits for them, and re-layouts: 9.54 us -> none
    all_to_all x2 -> x0, waiting for transfers between devices: 8.41 us -> none  [the longest x1 4.97 us: per_device(): lax.all_to_all(lax.all_to_all(cross_spectra, 'freq', split_axis=1, concat...]
    all_to_all x2 -> x0, starting transfers between devices: 6.83 us -> none  [the longest x1 3.49 us: per_device(): lax.all_to_all(lax.all_to_all(cross_spectra, 'freq', split_axis=1, concat...]
  transfers between devices with their start and end apart: 2 -> 0, of which waited for: 2 -> 0; matrix products, arithmetic and copies ran while one was open for 1% -> 0% of each run, Pallas kernels for 0% -> 0%
where the time goes in v1:
time: 29.1 us; the launch traced here: 28.9 us
  Pallas kernels  27.6 us (95%)
  local copies, waits for them, and re-layouts  1.26 us (4%)
    pallas_call x1, Pallas kernels, per_device(): pl.pallas_call(functools.partial(kernel, nf, ng), out_shape=jax.ShapeDtyp...  27.6 us
    unnamed x1, local copies, waits for them, and re-layouts  1.26 us

profile of v1, /device:TPU:0, one launch (start us, length us, event | category | flops | bytes accessed | tf_op | source)
XLA Modules:
  0.0 28.9 jit_solution(11667290594716874142)
XLA Ops:
  0.0 27.6 %shard_map.64 = f32[4,128]{1,0:T(4,128)} custom-call(f32[2,32,16,128]{3,2,1,0:T(8,128)} %spectra_hbm.1, f32[2,96,128]{2,1,0:T(8,128)} %sensor_hbm.1, f32[2,96,128]{2,1,0:T(8,128)} %source_hbm.1, f32[2,96]{1,0:T(2,128)} %wave_ref.1, f32[2,96]{1,0:T(2,128)} %atten_ref.1, s32[2]{0:T(128)} %counts_ref.1), custom_call_target="tpu_custom_call" | custom-call | tf_op jit(solution)/shard_map/pallas_call | solution.py:247
  27.6 1.3 %copy.8 = f32[4,128]{1,0:T(4,128)} copy(f32[4,128]{1,0:T(4,128)} %shard_map.64) | data formatting | bytes 4096

commit v2 on v1

--- a/solution.py
+++ b/solution.py
@@ -9,6 +9,7 @@
 
 RANGES = 64
 BLOCK = 8
+STEP = 2
 LANES = 128
 
 HIGH = lax.Precision.HIGHEST
@@ -96,7 +97,7 @@
         piece(k).start()
         return carry
 
-    lax.fori_loop(1, devices, send_piece, 0)
+    lax.fori_loop(1, devices, lambda k, c: send_piece(devices - k, c), 0)
 
     for b in range(nb):
         row = my_g * nb + b
@@ -115,6 +116,23 @@
             for blk in range(ranges // BLOCK):
                 cols_scr[b, i, blk] = turned[0:modes, blk * BLOCK : (blk + 1) * BLOCK]
 
+    for b in range(nb):
+
+        def pair_block(blk, carry):
+            first = pl.multiple_of(blk * BLOCK, BLOCK)
+            row_real = rows_scr[b, 0, pl.ds(first, BLOCK), :]
+            row_imag = rows_scr[b, 1, pl.ds(first, BLOCK), :]
+            col_real, col_imag = cols_scr[b, 0, blk], cols_scr[b, 1, blk]
+            for k in range(BLOCK):
+                nr, ni = row_real[k : k + 1, :], row_imag[k : k + 1, :]
+                mr = jnp.broadcast_to(col_real[:, k : k + 1], (modes, LANES))
+                mi = jnp.broadcast_to(col_imag[:, k : k + 1], (modes, LANES))
+                u_scr[b, first + k] = mr * nr + mi * ni
+                v_scr[b, first + k] = mr * ni - mi * nr
+            return carry
+
+        lax.fori_loop(0, ranges // BLOCK, pair_block, 0)
+
     own_shapes.wait()
     own_sources.wait()
     for k in range(1, ng):
@@ -133,14 +151,14 @@
             halves[b, LANES : LANES + modes, at] = rounded
             weight[b, :, at] = 2.0 * exact - rounded.astype(jnp.float32)
 
-    def put(k, block):
+    def put(i, k, block):
         high = block.astype(jnp.bfloat16)
         low = (block - high.astype(jnp.float32)).astype(jnp.bfloat16)
-        lhs[k * modes : (k + 1) * modes, 0:LANES] = high
-        lhs[k * modes : (k + 1) * modes, LANES : 2 * LANES] = low
-
-    def forms(b):
-        image = jnp.dot(lhs[...], halves[b], preferred_element_type=jnp.float32)
+        lhs[i, k * modes : (k + 1) * modes, 0:LANES] = high
+        lhs[i, k * modes : (k + 1) * modes, LANES : 2 * LANES] = low
+
+    def forms(i, b):
+        image = jnp.dot(lhs[i], halves[b], preferred_element_type=jnp.float32)
         image = image.reshape(BLOCK, modes, image.shape[1]) * weight[b][None]
         return jnp.sum(image, axis=1)
 
@@ -150,23 +168,15 @@
             wide[0:modes], wide, NT, precision=HIGH, preferred_element_type=jnp.float32
         )
 
-        def denom_block(blk, carry):
-            first = pl.multiple_of(blk * BLOCK, BLOCK)
-            row_real = rows_scr[b, 0, pl.ds(first, BLOCK), :]
-            row_imag = rows_scr[b, 1, pl.ds(first, BLOCK), :]
-            col_real, col_imag = cols_scr[b, 0, blk], cols_scr[b, 1, blk]
-            for k in range(BLOCK):
-                nr, ni = row_real[k : k + 1, :], row_imag[k : k + 1, :]
-                mr = jnp.broadcast_to(col_real[:, k : k + 1], (modes, LANES))
-                mi = jnp.broadcast_to(col_imag[:, k : k + 1], (modes, LANES))
-                u = mr * nr + mi * ni
-                u_scr[b, first + k] = u
-                v_scr[b, first + k] = mr * ni - mi * nr
-                put(k, gram * u)
-            denom[b, pl.ds(first, BLOCK), :] = forms(b)
+        def denom_step(step, carry):
+            for i in range(STEP):
+                first = pl.multiple_of((step * STEP + i) * BLOCK, BLOCK)
+                for k in range(BLOCK):
+                    put(i, k, gram * u_scr[b, first + k])
+                denom[b, pl.ds(first, BLOCK), :] = forms(i, b) * float(bins)
             return carry
 
-        lax.fori_loop(0, ranges // BLOCK, denom_block, 0)
+        lax.fori_loop(0, ranges // BLOCK // STEP, denom_step, 0)
 
     def take_piece(k, carry):
         piece(k).wait_recv()
@@ -183,22 +193,25 @@
         even = (0.5 * (full + turned))[0:modes]
         odd = (0.5 * (full - turned))[0:modes]
 
-        def numer_block(blk, carry):
-            first = pl.multiple_of(blk * BLOCK, BLOCK)
-            for k in range(BLOCK):
-                put(k, even * u_scr[b, first + k] - odd * v_scr[b, first + k])
-            score = forms(b) / (denom[b, pl.ds(first, BLOCK), :] * float(bins))
-            for g in range(ng):
-                for s in range(BLOCK // share):
-                    value = score[s * share : (s + 1) * share, g * depth_here : (g + 1) * depth_here]
-                    slot = blk * (BLOCK // share) + s
-                    if b == 0:
-                        power[g, slot] = value
-                    else:
-                        power[g, slot] += value
+        def numer_step(step, carry):
+            for i in range(STEP):
+                blk = step * STEP + i
+                first = pl.multiple_of(blk * BLOCK, BLOCK)
+                for k in range(BLOCK):
+                    put(i, k, even * u_scr[b, first + k] - odd * v_scr[b, first + k])
+                score = forms(i, b) / denom[b, pl.ds(first, BLOCK), :]
+                for g in range(ng):
+                    for t in range(BLOCK // share):
+                        at = slice(g * depth_here, (g + 1) * depth_here)
+                        value = score[t * share : (t + 1) * share, at]
+                        slot = blk * (BLOCK // share) + t
+                        if b == 0:
+                            power[g, slot] = value
+                        else:
+                            power[g, slot] += value
             return carry
 
-        lax.fori_loop(0, ranges // BLOCK, numer_block, 0)
+        lax.fori_loop(0, ranges // BLOCK // STEP, numer_step, 0)
 
     def part(k):
         peer = lax.rem(me + k, devices)
@@ -265,7 +278,7 @@
                 pltpu.VMEM((8, LANES), f32),
                 pltpu.VMEM((nb, ranges, modes, LANES), f32),
                 pltpu.VMEM((nb, ranges, modes, LANES), f32),
-                pltpu.VMEM((BLOCK * modes, 2 * LANES), bf16),
+                pltpu.VMEM((STEP, BLOCK * modes, 2 * LANES), bf16),
                 pltpu.VMEM((nb, ranges, ng * depth_here), f32),
                 pltpu.VMEM((ng, nf, share, depth_here), f32),
                 pltpu.VMEM((devices, share, depth_here), f32),

time: 29.1 us -> 26.2 us (0.900)
  Pallas kernels: 27.6 us -> 24.7 us
    pallas_call x1, Pallas kernels: 27.6 us -> 24.7 us  [per_device(): pl.pallas_call(functools.partial(kernel, nf, ng), out_shape=jax.ShapeDtyp...]
where the time goes in v2:
time: 26.2 us; the launch traced here: 26 us
  Pallas kernels  24.7 us (94%)
  local copies, waits for them, and re-layouts  1.26 us (5%)
    pallas_call x1, Pallas kernels, per_device(): pl.pallas_call(functools.partial(kernel, nf, ng), out_shape=jax.ShapeDtyp...  24.7 us
    unnamed x1, local copies, waits for them, and re-layouts  1.26 us

profile of v2, /device:TPU:0, one launch (start us, length us, event | category | flops | bytes accessed | tf_op | source)
XLA Modules:
  0.0 26.0 jit_solution(15769386817404437902)
XLA Ops:
  0.0 24.7 %shard_map.64 = f32[4,128]{1,0:T(4,128)} custom-call(f32[2,32,16,128]{3,2,1,0:T(8,128)} %spectra_hbm.1, f32[2,96,128]{2,1,0:T(8,128)} %sensor_hbm.1, f32[2,96,128]{2,1,0:T(8,128)} %source_hbm.1, f32[2,96]{1,0:T(2,128)} %wave_ref.1, f32[2,96]{1,0:T(2,128)} %atten_ref.1, s32[2]{0:T(128)} %counts_ref.1), custom_call_target="tpu_custom_call" | custom-call | tf_op jit(solution)/shard_map/pallas_call | solution.py:260
  24.7 1.3 %copy.8 = f32[4,128]{1,0:T(4,128)} copy(f32[4,128]{1,0:T(4,128)} %shard_map.64) | data formatting | bytes 4096

commit v3 on v2

--- a/solution.py
+++ b/solution.py
@@ -9,12 +9,22 @@
 
 RANGES = 64
 BLOCK = 8
-STEP = 2
+STEP = 8
 LANES = 128
 
 HIGH = lax.Precision.HIGHEST
 MESH = pl.DeviceIdType.MESH
 NT = (((1,), (1,)), ((), ()))
+NN = (((1,), (0,)), ((), ()))
+
+
+def split(value):
+    high = value.astype(jnp.bfloat16)
+    return high, (value - high.astype(jnp.float32)).astype(jnp.bfloat16)
+
+
+def product(left, right, dims):
+    return lax.dot_general(left, right, dims, preferred_element_type=jnp.float32)
 
 
 def kernel(
@@ -178,6 +188,29 @@
 
         lax.fori_loop(0, ranges // BLOCK // STEP, denom_step, 0)
 
+    def part(peer, slot):
+        peer_f, peer_g = peer // ng, lax.rem(peer, ng)
+        return pltpu.make_async_remote_copy(
+            src_ref=power.at[peer_g, peer_f],
+            dst_ref=parts.at[slot],
+            send_sem=part_send.at[peer],
+            recv_sem=part_recv.at[slot],
+            device_id=(peer_f, peer_g),
+            device_id_type=MESH,
+        )
+
+    blocks = ranges // BLOCK
+    owners = BLOCK // share
+    low = 1 - (my_f // owners * 2) // blocks
+
+    def block_at(n):
+        return lax.rem(my_f // owners + (1 - 2 * low) * (n + 1) + blocks, blocks)
+
+    def send_block(n):
+        for t in range(owners):
+            for g in range(ng):
+                part((block_at(n) * owners + t) * ng + g, me).start()
+
     def take_piece(k, carry):
         piece(k).wait_recv()
         return carry
@@ -187,54 +220,60 @@
     for b in range(nb):
         wide = shapes_wide[b]
         whole = jnp.concatenate([table[g, b] for g in range(ng)], axis=1)
-        half = jnp.dot(wide, whole, precision=HIGH, preferred_element_type=jnp.float32)
-        full = lax.dot_general(half, wide, NT, precision=HIGH, preferred_element_type=jnp.float32)
+        left_high, left_low = split(wide)
+        mid_high, mid_low = split(whole)
+        both = jnp.concatenate([left_high, left_low], 0)
+        half = product(both, mid_high, NN)
+        half = half[:LANES] + (half[LANES:] + product(left_high, mid_low, NN))
+        half_high, half_low = split(half)
+        both = jnp.concatenate([half_high, half_low], 0)
+        full = product(both, left_high, NT)
+        full = full[:LANES] + (full[LANES:] + product(half_high, left_low, NT))
         turned = full.T
         even = (0.5 * (full + turned))[0:modes]
         odd = (0.5 * (full - turned))[0:modes]
 
         def numer_step(step, carry):
             for i in range(STEP):
-                blk = step * STEP + i
+                blk = block_at(step * STEP + i)
                 first = pl.multiple_of(blk * BLOCK, BLOCK)
                 for k in range(BLOCK):
                     put(i, k, even * u_scr[b, first + k] - odd * v_scr[b, first + k])
                 score = forms(i, b) / denom[b, pl.ds(first, BLOCK), :]
                 for g in range(ng):
-                    for t in range(BLOCK // share):
+                    for t in range(owners):
                         at = slice(g * depth_here, (g + 1) * depth_here)
                         value = score[t * share : (t + 1) * share, at]
-                        slot = blk * (BLOCK // share) + t
+                        slot = blk * owners + t
                         if b == 0:
                             power[g, slot] = value
                         else:
                             power[g, slot] += value
+                if b == nb - 1 and i > 0:
+                    send_block(step * STEP + i - 1)
+                elif b == nb - 1:
+
+                    @pl.when(step > 0)
+                    def _():
+                        send_block(step * STEP - 1)
+
             return carry
 
         lax.fori_loop(0, ranges // BLOCK // STEP, numer_step, 0)
 
-    def part(k):
-        peer = lax.rem(me + k, devices)
-        peer_f, peer_g = peer // ng, lax.rem(peer, ng)
-        return pltpu.make_async_remote_copy(
-            src_ref=power.at[peer_g, peer_f],
-            dst_ref=parts.at[k],
-            send_sem=part_send.at[k],
-            recv_sem=part_recv.at[k],
-            device_id=(peer_f, peer_g),
-            device_id_type=MESH,
-        )
-
-    def send_part(k, carry):
-        part(k).start()
-        return carry
-
-    lax.fori_loop(1, devices, send_part, 0)
-    parts[0] = power[my_g, my_f]
+    def send_last(k, carry):
+        peer = me // (owners * ng) * (owners * ng) + lax.rem(me + k, owners * ng)
+        part(peer, me).start()
+        return carry
+
+    lax.fori_loop(1, owners * ng, send_last, 0)
+    parts[me] = power[my_g, my_f]
 
     def finish(k, carry):
         piece(k).wait_send()
-        part(k).wait()
+        peer = lax.rem(me + k, devices)
+        part(peer, me).wait_send()
+        part(peer, peer).wait_recv()
         return carry
 
     for k in range(1, ng):

time: 26.2 us -> 25.6 us (0.977)
  Pallas kernels: 24.7 us -> 24.2 us
    pallas_call x1, Pallas kernels: 24.7 us -> 24.2 us  [per_device(): pl.pallas_call(functools.partial(kernel, nf, ng), out_shape=jax.ShapeDtyp...]
where the time goes in v3:
time: 25.6 us; the launch traced here: 25.4 us
  Pallas kernels  24.2 us (95%)
  local copies, waits for them, and re-layouts  1.26 us (5%)
    pallas_call x1, Pallas kernels, per_device(): pl.pallas_call(functools.partial(kernel, nf, ng), out_shape=jax.ShapeDtyp...  24.2 us
    unnamed x1, local copies, waits for them, and re-layouts  1.26 us

profile of v3, /device:TPU:0, one launch (start us, length us, event | category | flops | bytes accessed | tf_op | source)
XLA Modules:
  0.0 25.4 jit_solution(2453478127714008832)
XLA Ops:
  0.0 24.2 %shard_map.64 = f32[4,128]{1,0:T(4,128)} custom-call(f32[2,32,16,128]{3,2,1,0:T(8,128)} %spectra_hbm.1, f32[2,96,128]{2,1,0:T(8,128)} %sensor_hbm.1, f32[2,96,128]{2,1,0:T(8,128)} %source_hbm.1, f32[2,96]{1,0:T(2,128)} %wave_ref.1, f32[2,96]{1,0:T(2,128)} %atten_ref.1, s32[2]{0:T(128)} %counts_ref.1), custom_call_target="tpu_custom_call" | custom-call | tf_op jit(solution)/shard_map/pallas_call | solution.py:299
  24.2 1.3 %copy.8 = f32[4,128]{1,0:T(4,128)} copy(f32[4,128]{1,0:T(4,128)} %shard_map.64) | data formatting | bytes 4096
